TPU v7x, 32 devices: a whole 2x2x4 slice. The times are simulated.
32 devices in a mesh: bank: 4 (over x, core), zero: 8 (over z, y).
Axes of the slice: x: 2, y: 2, z: 4, core: 2. Of those that a mesh axis runs over, the one named last changes fastest.
Arguments:
- w_gate: float32 [64, 2048, 1024], P('bank', 'zero'), may hold values from -0.1875 to 0.1875
- avg_gate: float32 [64, 2048, 1024], P('bank', 'zero'), may hold values from -0.125 to 0.125
- w_up: float32 [64, 2048, 1024], P('bank', 'zero'), may hold values from -0.1875 to 0.1875
- avg_up: float32 [64, 2048, 1024], P('bank', 'zero'), may hold values from -0.125 to 0.125
- mix_share: float32 [64], P('bank'), may hold values from 0.2 to 0.8
- router_weight: float32 [2048, 64], P('zero', 'bank'), may hold values from -0.125 to 0.125
- router_gain: float32 [2048], P('zero'), may hold values from 0.25 to 1.75
Outputs:
- serve_gate: bfloat16 [64, 2048, 1024], P('bank', None, 'zero')
- serve_up: bfloat16 [64, 2048, 1024], P('bank', None, 'zero')
- scale_gate: float32 [64, 1024], P('bank', 'zero')
- scale_up: float32 [64, 1024], P('bank', 'zero')
- serve_router: bfloat16 [2048, 64], replicated
All inputs are finite; a program needn't handle non-finite values. Where the computation divides by a largest or mean magnitude, that divisor is 1e-20 or more.
Results may differ from a plain program's by a relative error of at most 0.001.
Values may be sent and summed in bfloat16 or wider, within the bound.
A program may use at most 256 MiB of HBM per device.

v0:
```python
import functools

import jax
import jax.numpy as jnp
from jax import lax
from jax.experimental import pallas as pl
from jax.experimental.pallas import tpu as pltpu
from jax.sharding import PartitionSpec as P

MESH = pl.DeviceIdType.MESH
SLOTS = 4


def partner(me, k, n):
    out, bit = me, 1
    while bit < n:
        if k & bit:
            out = out + bit * (1 - 2 * ((me // bit) % 2))
        bit *= 2
    return out


def plan(experts):
    first = max(1, experts // 16)
    sizes = [first, 3 * first, experts - 4 * first]
    groups, at, row = [], 0, 0
    for i, size in enumerate(sizes):
        if i == 0:
            cuts = [size]
        elif i == 1:
            cuts = [first] * 3
        else:
            step = max(1, size // 3)
            cuts = [step, step, size - 2 * step]
        pieces, p = [], at
        for c in cuts:
            if c > 0:
                pieces.append((p, c))
                p += c
        rows = -(-2 * size // 8) * 8
        groups.append((at, size, row, rows, pieces))
        at += size
        row += rows
    return groups, row


def kernel(
    nz, nb, groups,
    mix, wg, ag, wu, au, rw, gain,
    og, ou, sg, su, rt,
    fresh, stage, send, part, rs, scl, rtp,
    in_sem, bulk_ssem, bulk_rsem, own_sem, rs_ssem, rs_rsem, ag_ssem, ag_rsem,
    r1_ssem, r1_rsem, r2_ssem, r2_rsem, r_own,
):
    me = lax.axis_index("zero")
    bank = lax.axis_index("bank")
    experts, rows, _ = wg.shape
    cb = part.shape[2]
    eb = rw.shape[0]
    ws, avgs, outs, scales = (wg, wu), (ag, au), (og, ou), (sg, su)
    peers = [partner(me, k, nz) for k in range(1, nz)]
    banks = [partner(bank, k, nb) for k in range(1, nb)]

    def loads(e):
        slot = lax.rem(e, SLOTS)
        out = []
        for m in range(2):
            out.append(pltpu.make_async_copy(ws[m].at[e], fresh.at[m, e], in_sem.at[slot, m, 0]))
            out.append(pltpu.make_async_copy(avgs[m].at[e], stage.at[slot, m], in_sem.at[slot, m, 1]))
        return out

    for e in range(min(SLOTS, experts)):
        for c in loads(e):
            c.start()

    barrier = pltpu.get_barrier_semaphore()
    for p in peers:
        pl.semaphore_signal(barrier, inc=1, device_id={"zero": p}, device_id_type=MESH)
    for p in banks:
        pl.semaphore_signal(barrier, inc=1, device_id={"bank": p}, device_id_type=MESH)

    part[...] = jnp.zeros_like(part)
    rtp[...] = (rw[...] * gain[...]).astype(rtp.dtype)

    def compute(g):
        at, size, row0, _, _ = groups[g]

        def body(e, carry):
            slot = lax.rem(e, SLOTS)
            for c in loads(e):
                c.wait()
            a = mix[e]
            b = 1.0 - a
            for m in range(2):
                row = row0 + m * size + (e - at)
                for d in range(nz):
                    cols = slice(d * cb, (d + 1) * cb)
                    v = a * fresh[m, e, :, cols] + b * stage[slot, m, :, cols]
                    fresh[m, e, :, cols] = v
                    part[d, pl.ds(row, 1), :] = jnp.sum(jnp.abs(v), axis=0, keepdims=True)

            @pl.when(e + SLOTS < experts)
            def _():
                for c in loads(e + SLOTS):
                    c.start()

            return carry

        lax.fori_loop(at, at + size, body, 0)

    def scatter(g):
        _, _, row0, n, _ = groups[g]
        span = pl.ds(row0, n)
        out = []
        for k, p in enumerate(peers):
            out.append(pltpu.make_async_remote_copy(
                part.at[p, span], rs.at[k, span], rs_ssem.at[g, k], rs_rsem.at[g, k],
                device_id={"zero": p}, device_id_type=MESH))
            out[-1].start()
        return out

    def gather(g, pending):
        at, size, row0, n, _ = groups[g]
        span = pl.ds(row0, n)
        for c in pending:
            c.wait()
        total = part[me, span, :]
        for k in range(nz - 1):
            total = total + rs[k, span, :]
        total = total / (rows * nz)
        scl[me, span, :] = total
        for m in range(2):
            scales[m][at:at + size, :] = total[m * size:(m + 1) * size, :]
        out = []
        for k, p in enumerate(peers):
            out.append(pltpu.make_async_remote_copy(
                scl.at[me, span], scl.at[me, span], ag_ssem.at[g, k], ag_rsem.at[g, k],
                device_id={"zero": p}, device_id_type=MESH))
            out[-1].start()
        return out

    def narrow(g, lo, n):
        at, size, row0, _, _ = groups[g]

        def body(e, carry):
            for m in range(2):
                row = row0 + m * size + (e - at)
                for d in range(nz):
                    cols = slice(d * cb, (d + 1) * cb)
                    inverse = 1.0 / scl[d, pl.ds(row, 1), :]
                    send[m, d, e] = (fresh[m, e, :, cols] * inverse).astype(send.dtype)
            return carry

        lax.fori_loop(lo, lo + n, body, 0)

    place = pl.ds(pl.multiple_of(me * rows, rows), rows)
    flying = []
    count = [0]

    def push(lo, n):
        i = count[0]
        count[0] += 1
        span = pl.ds(lo, n)
        for k, p in enumerate(peers):
            for m in range(2):
                c = pltpu.make_async_remote_copy(
                    send.at[m, p, span], outs[m].at[span, place], bulk_ssem.at[i, m, k], bulk_rsem.at[i, m, k],
                    device_id={"zero": p}, device_id_type=MESH)
                c.start()
                flying.append(c)
        for m in range(2):
            c = pltpu.make_async_copy(send.at[m, me, span], outs[m].at[span, place], own_sem.at[i, m])
            c.start()
            flying.append(c)

    compute(0)
    pl.semaphore_wait(barrier, nz - 1 + nb - 1)
    rs0 = scatter(0)
    band = pl.ds(pl.multiple_of(bank * eb, eb), eb)
    if len(rt.shape) == 2:
        mine, column = rt.at[band, place], rt.at[band]
    else:
        mine, column = rt.at[me, band], rt.at[:, band]
    first = []
    for k, p in enumerate(peers):
        first.append(pltpu.make_async_remote_copy(
            rtp, mine, r1_ssem.at[k], r1_rsem.at[k], device_id={"zero": p}, device_id_type=MESH))
    first.append(pltpu.make_async_copy(rtp, mine, r_own))
    compute(1)
    rs1 = scatter(1)
    ag0 = gather(0, rs0)
    ag1 = gather(1, rs1)
    for c in first:
        c.start()
    for c in ag0:
        c.wait()
    for lo, n in groups[0][4]:
        narrow(0, lo, n)
        push(lo, n)
    for c in ag1:
        c.wait()
    early, middle, late = groups[1][4]
    narrow(1, *early)
    push(*early)
    compute(2)
    rs2 = scatter(2)
    narrow(1, *middle)
    push(*middle)
    narrow(1, *late)
    for c in first:
        c.wait()
    for k, p in enumerate(banks):
        c = pltpu.make_async_remote_copy(
            column, column, r2_ssem.at[k], r2_rsem.at[k], device_id={"bank": p}, device_id_type=MESH)
        c.start()
        flying.append(c)
    ag2 = gather(2, rs2)
    push(*late)
    for c in ag2:
        c.wait()
    for lo, n in groups[2][4]:
        narrow(2, lo, n)
        push(lo, n)
    for c in flying:
        c.wait()


def settle(count, *refs):
    sources, targets, buffers = refs[:count], refs[count:2 * count], refs[2 * count:3 * count]
    big_in, big_out, small_in, small_out = refs[3 * count:]
    jobs = []
    for i in range(2):
        for e in range(sources[i].shape[0]):
            jobs.append((sources[i].at[e], buffers[i].at[e], targets[i].at[e], big_in.at[i, e], big_out.at[i, e]))
    for i in range(2, count):
        jobs.append((sources[i], buffers[i], targets[i], small_in.at[i - 2], small_out.at[i - 2]))
    reads = [pltpu.make_async_copy(src, buf, sem) for src, buf, _, sem, _ in jobs]
    writes = [pltpu.make_async_copy(buf, dst, sem) for _, buf, dst, _, sem in jobs]
    for r in reads:
        r.start()
    for r, w in zip(reads, writes):
        r.wait()
        w.start()
    for w in writes:
        w.wait()


def solution(mesh):
    nz, nb = mesh.shape["zero"], mesh.shape["bank"]

    def on_device(w_gate, avg_gate, w_up, avg_up, mix_share, router_weight, router_gain):
        experts, rows, columns = w_gate.shape
        cb = columns // nz
        eb = router_weight.shape[1]
        groups, stat = plan(experts)
        npieces = sum(len(g[4]) for g in groups)
        anyspace = pl.BlockSpec(memory_space=pl.ANY)
        vmem = pl.BlockSpec(memory_space=pltpu.VMEM)
        dma = pltpu.SemaphoreType.DMA
        out = jax.ShapeDtypeStruct((experts, rows * nz, cb), jnp.bfloat16)
        scale = jax.ShapeDtypeStruct((experts, cb), jnp.float32)
        flat = rows % 128 == 0
        router = (eb * nb, rows * nz) if flat else (nz, eb * nb, rows)
        router = jax.ShapeDtypeStruct(router, jnp.bfloat16)
        ng = len(groups)
        landed = pl.pallas_call(
            functools.partial(kernel, nz, nb, groups),
            out_shape=(out, out, scale, scale, router),
            in_specs=[pl.BlockSpec(memory_space=pltpu.SMEM)] + [anyspace] * 4 + [vmem] * 2,
            out_specs=(anyspace, anyspace, vmem, vmem, anyspace),
            scratch_shapes=[
                pltpu.VMEM((2, experts, rows, columns), jnp.float32),
                pltpu.VMEM((SLOTS, 2, rows, columns), jnp.float32),
                pltpu.VMEM((2, nz, experts, rows, cb), jnp.bfloat16),
                pltpu.VMEM((nz, stat, cb), jnp.float32),
                pltpu.VMEM((nz - 1, stat, cb), jnp.float32),
                pltpu.VMEM((nz, stat, cb), jnp.float32),
                pltpu.VMEM((eb, rows), jnp.bfloat16),
                dma((SLOTS, 2, 2)),
                dma((npieces, 2, nz - 1)),
                dma((npieces, 2, nz - 1)),
                dma((npieces, 2)),
                dma((ng, nz - 1)),
                dma((ng, nz - 1)),
                dma((ng, nz - 1)),
                dma((ng, nz - 1)),
                dma((nz - 1,)),
                dma((nz - 1,)),
                dma((nb - 1,)),
                dma((nb - 1,)),
                dma,
            ],
            compiler_params=pltpu.CompilerParams(
                collective_id=0, has_side_effects=True, vmem_limit_bytes=67_000_000
            ),
        )(mix_share, w_gate, avg_gate, w_up, avg_up, router_weight.T, router_gain[None, :])
        shapes = (out, out, scale, scale, router)
        sg, su, cg, cu, rt = pl.pallas_call(
            functools.partial(settle, len(shapes)),
            out_shape=shapes,
            in_specs=[anyspace] * len(shapes),
            out_specs=(anyspace,) * len(shapes),
            scratch_shapes=[pltpu.VMEM(x.shape, x.dtype) for x in shapes]
            + [dma((2, experts))] * 2
            + [dma((len(shapes) - 2,))] * 2,
            compiler_params=pltpu.CompilerParams(vmem_limit_bytes=60_000_000),
        )(*landed)
        rt = rt.T if flat else rt.transpose(0, 2, 1).reshape(nz * rows, nb * eb)
        return sg, su, cg, cu, rt

    in_specs = (
        P("bank", "zero", None),
        P("bank", "zero", None),
        P("bank", "zero", None),
        P("bank", "zero", None),
        P("bank"),
        P("zero", "bank"),
        P("zero"),
    )
    out_specs = (
        P("bank", None, "zero"),
        P("bank", None, "zero"),
        P("bank", "zero"),
        P("bank", "zero"),
        P(),
    )
    return jax.shard_map(
        on_device, mesh=mesh, in_specs=in_specs, out_specs=out_specs, check_vma=False
    )
```

profile of v0, /device:TPU:8, one launch (start us, length us, event | category | flops | bytes accessed | tf_op | source)
XLA Modules:
  0.0 396.0 jit_solution(10927004967650237481)
XLA Ops:
  0.6 382.8 %shard_map.110 = (bf16[16,2048,128]{2,1,0:T(8,128)(2,1)}, bf16[16,2048,128]{2,1,0:T(8,128)(2,1)}, f32[16,128]{1,0:T(8,128)}, f32[16,128]{1,0:T(8,128)}, bf16[64,2048]{1,0:T(8,128)(2,1)}) custom-call(f32[16]{0:T(128)} %mix.1, f32[16,256,1024]{2,1,0:T(8,128)} %wg.1, f32[16,256,1024]{2,1,0:T(8,128)} %ag.1, f32[16,256,1024]{2,1,0:T(8,128)} %wu.1, ...), custom_call_target="tpu_custom_call" | custom-call | tf_op jit(solution)/shard_map/pallas_call | solution.py:266
  383.5 12.5 %shard_map.111 = (bf16[16,2048,128]{2,1,0:T(8,128)(2,1)}, bf16[16,2048,128]{2,1,0:T(8,128)(2,1)}, f32[16,128]{1,0:T(8,128)}, f32[16,128]{1,0:T(8,128)}, bf16[64,2048]{1,0:T(8,128)(2,1)}) custom-call(bf16[16,2048,128]{2,1,0:T(8,128)(2,1)} %get-tuple-element.15.refs_0_, bf16[16,2048,128]{2,1,0:T(8,128)(2,1)} %get-tuple-element.16.refs_1_, ...), custom_call_target="tpu_custom_call" | custom-call | tf_op jit(solution)/shard_map/pallas_call | solution.py:298
where the time goes:
time: 396 us
  Pallas kernels  395 us (100%)
    pallas_call x1, Pallas kernels, on_device(): pl.pallas_call(functools.partial(kernel, nz, nb, groups), out_shape=(out,...  383 us
    pallas_call x1, Pallas kernels, on_device(): pl.pallas_call(functools.partial(settle, len(shapes)), out_shape=shapes,...  12.5 us

commit v1 on v0

v1 whole, which is shorter than its diff:
```python
import functools

import jax
import jax.numpy as jnp
from jax import lax
from jax.experimental import pallas as pl
from jax.experimental.pallas import tpu as pltpu
from jax.sharding import PartitionSpec as P

MESH = pl.DeviceIdType.MESH
HEAD = 3
RING = 2
STEP = 32


def partner(me, k, n):
    out, bit = me, 1
    while bit < n:
        if k & bit:
            out = out + bit * (1 - 2 * ((me // bit) % 2))
        bit *= 2
    return out


def kernel(
    nz, nb, head,
    mix_in, wg, ag, wu, au, rw_in, gain_in,
    land, scl, rt,
    mix, rw, gain, stage, send, pa, ra, sa, part, rs, half, other, sb, rtp,
    small_sem, in_sem, pa_ssem, pa_rsem, step_ssem, step_rsem, bulk_ssem, bulk_rsem, r_ssem, r_rsem,
):
    me = lax.axis_index("zero")
    bank = lax.axis_index("bank")
    experts, rows, _ = wg.shape
    cb = land.shape[3]
    eb = rw.shape[0]
    tail = experts - head
    nh = nz // 2
    near = lax.rem(me, nh)
    ws, avgs = (wg, wu), (ag, au)
    peers = [partner(me, k, nz) for k in range(1, nz)]
    inner, far = peers[:nh - 1], peers[nh - 1]
    banks = [partner(bank, k, nb) for k in range(1, nb)]

    def loads(e, slot):
        for m in range(2):
            for i, source in enumerate((ws[m], avgs[m])):
                pltpu.make_async_copy(source.at[e], stage.at[slot, m, i], in_sem.at[slot]).start()

    def loaded(slot):
        pltpu.make_async_copy(stage.at[slot], stage.at[slot], in_sem.at[slot]).wait()

    def to(p, source, target, ssem, rsem):
        pltpu.make_async_remote_copy(
            source, target, ssem, rsem, device_id={"zero": p}, device_id_type=MESH).start()

    def sent(ref, sem):
        pltpu.make_async_copy(ref, ref, sem).wait()

    small = [
        pltpu.make_async_copy(mix_in, mix, small_sem.at[0]),
        pltpu.make_async_copy(rw_in, rw, small_sem.at[1]),
        pltpu.make_async_copy(gain_in, gain, small_sem.at[2]),
    ]
    small[0].start()
    for e in range(head):
        loads(e, e)

    barrier = pltpu.get_barrier_semaphore()
    for p in peers:
        pl.semaphore_signal(barrier, inc=1, device_id={"zero": p}, device_id_type=MESH)
    for p in banks:
        pl.semaphore_signal(barrier, inc=1, device_id={"bank": p}, device_id_type=MESH)
    for c in small[1:]:
        c.start()

    def ring(i):
        return head + lax.rem(i, RING)

    def fresh(slot, e, m, d, span):
        cols = slice(d * cb, (d + 1) * cb)
        a = mix[e]
        return a * stage[slot, m, 0, span, cols] + (1.0 - a) * stage[slot, m, 1, span, cols]

    def sizes_of(slot, e, m):
        def body(i, sums):
            span = pl.ds(pl.multiple_of(i * STEP, STEP), STEP)
            out = []
            for d in range(nz):
                v = jnp.abs(fresh(slot, e, m, d, span))
                out.append(sums[d] + sum(v[j:j + 8] for j in range(0, STEP, 8)))
            return tuple(out)

        sums = lax.fori_loop(0, rows // STEP, body, tuple(jnp.zeros((8, cb), jnp.float32) for _ in range(nz)))
        return [jnp.sum(s, axis=0, keepdims=True) for s in sums]

    def head_sizes(e):
        loaded(e)
        for m in range(2):
            for d, size in enumerate(sizes_of(e, e, m)):
                pa[e, m, d:d + 1, :] = size

    def head_send(e):
        for k, p in enumerate(peers):
            to(p, pa.at[e], ra.at[e, k], pa_ssem.at[e], pa_rsem.at[e])

    def head_scale(e):
        sent(ra.at[e], pa_rsem.at[e])
        total = pa[e]
        for k in range(nz - 1):
            total = total + ra[e, k]
        sa[e] = total / (rows * nz)
        for m in range(2):
            scl[m, e:e + 1, :] = sa[e, m, pl.ds(me, 1), :]

    place = pl.ds(pl.multiple_of(me * rows, rows), rows)

    def narrow(slot, e, m, scale):
        inverses = [1.0 / scale(m, d) for d in range(nz)]

        def body(i, carry):
            span = pl.ds(pl.multiple_of(i * STEP, STEP), STEP)
            for d in range(nz):
                send[m, d, e, span, :] = (fresh(slot, e, m, d, span) * inverses[d]).astype(send.dtype)
            return carry

        lax.fori_loop(0, rows // STEP, body, 0)

    def push(e, m):
        land[m, e, place, :] = send[m, me, e]
        for p in peers:
            to(p, send.at[m, p, e], land.at[m, e, place], bulk_ssem, bulk_rsem)

    def tail_sizes(i, carry):
        e = head + i
        loaded(ring(i))
        for m in range(2):
            for d, size in enumerate(sizes_of(ring(i), e, m)):
                part[d // nh, d % nh, pl.ds(m * tail + i, 1), :] = size

        @pl.when(i + RING < tail)
        def _():
            loads(e + RING, ring(i))

        return carry

    small[0].wait()
    head_sizes(0)
    for i in range(min(RING, tail)):
        loads(head + i, ring(i))
    pl.semaphore_wait(barrier, nz - 1 + nb - 1)
    head_send(0)
    for c in small[1:]:
        c.wait()
    rtp[...] = (rw[...] * gain[...]).astype(rtp.dtype)
    band = pl.ds(pl.multiple_of(bank * eb, eb), eb)
    flat = len(rt.shape) == 2
    if flat:
        mine = rt.at[band, place]
        theirs = rt.at[band, pl.ds(pl.multiple_of(far * rows, rows), rows)]
        tiles = rt.at[band, pl.ds(0, 2 * (nh - 1) * rows)]
        column = rt.at[band]
        others = rt.at[pl.ds(0, (nb - 1) * eb)]
        rt[band, place] = rtp[...]
    else:
        mine = rt.at[me, band]
        theirs = rt.at[far, band]
        tiles = rt.at[pl.ds(0, 2 * (nh - 1)), band]
        column = rt.at[:, band]
        others = rt.at[:, pl.ds(0, (nb - 1) * eb)]
        rt[me, band] = rtp[...]
    to(far, rtp, mine, r_ssem.at[0], r_rsem.at[0])
    for e in range(1, head):
        head_sizes(e)
        head_send(e)
    part[:, :, 2 * tail:, :] = jnp.zeros_like(part[:, :, 2 * tail:, :])

    for e in range(head):
        head_scale(e)
        for m in range(2):
            narrow(e, e, m, lambda m, d, e=e: sa[e, m, d:d + 1, :])
            if e == 0:
                push(e, m)
    lax.fori_loop(0, tail, tail_sizes, 0)

    for k, p in enumerate(inner):
        to(p, part.at[:, lax.rem(p, nh)], rs.at[k], step_ssem.at[0], step_rsem.at[0])
    push(1, 0)
    for i in range(min(RING, tail)):
        loads(head + i, ring(i))
    pltpu.make_async_copy(theirs, theirs, r_rsem.at[0]).wait()
    for p in inner:
        for tile in (mine, theirs):
            to(p, tile, tile, r_ssem.at[1], r_rsem.at[1])

    sent(rs, step_rsem.at[0])
    total = part[:, near]
    for k in range(nh - 1):
        total = total + rs[k]
    half[...] = total
    to(far, half, other, step_ssem.at[1], step_rsem.at[1])
    push(1, 1)

    sent(other, step_rsem.at[1])
    total = (half[...] + other[...]) / (rows * nz)
    sb[:, near] = total
    for m in range(2):
        scl[m, head:, :] = sb[me // nh, near, m * tail:(m + 1) * tail, :]
    for p in inner:
        to(p, sb.at[:, near], sb.at[:, near], step_ssem.at[2], step_rsem.at[2])
    for e in range(2, head):
        for m in range(2):
            push(e, m)

    sent(tiles, r_rsem.at[1])
    for p in banks:
        pltpu.make_async_remote_copy(
            column, column, r_ssem.at[2], r_rsem.at[2], device_id={"bank": p}, device_id_type=MESH).start()
    sent(rs, step_rsem.at[2])

    def serve(i, carry):
        e = head + i
        loaded(ring(i))
        for m in range(2):
            narrow(ring(i), e, m, lambda m, d: sb[d // nh, d % nh, pl.ds(m * tail + i, 1), :])
            push(e, m)

        @pl.when(i + RING < tail)
        def _():
            loads(e + RING, ring(i))

        return carry

    lax.fori_loop(0, tail, serve, 0)

    for e in range(head):
        sent(ra.at[e], pa_ssem.at[e])
    sent(rs, step_ssem.at[0])
    sent(other, step_ssem.at[1])
    sent(rs, step_ssem.at[2])
    sent(rtp, r_ssem.at[0])
    sent(tiles, r_ssem.at[1])
    for sem in (r_ssem, r_rsem):
        sent(others, sem.at[2])
    sent(send.at[:, pl.ds(0, nz - 1)], bulk_ssem)
    sent(land.at[:, :, pl.ds(0, (nz - 1) * rows)], bulk_rsem)


def settle(land, scl, rt, og, ou, sg, su, out, sem):
    pairs = ((land.at[0], og), (land.at[1], ou), (scl.at[0], sg), (scl.at[1], su), (rt, out))
    for i, (source, target) in enumerate(pairs):
        if i < 2:
            for e in range(source.shape[0]):
                pltpu.make_async_copy(source.at[e], target.at[e], sem.at[i]).start()
        else:
            pltpu.make_async_copy(source, target, sem.at[i]).start()
    for i, (source, target) in enumerate(pairs):
        pltpu.make_async_copy(source, target, sem.at[i]).wait()


def solution(mesh):
    nz, nb = mesh.shape["zero"], mesh.shape["bank"]

    def on_device(w_gate, avg_gate, w_up, avg_up, mix_share, router_weight, router_gain):
        experts, rows, columns = w_gate.shape
        cb = columns // nz
        eb = router_weight.shape[1]
        nh = nz // 2
        head = min(HEAD, experts - 1)
        stat = (2 * (experts - head) // 8 + 1) * 8
        anyspace = pl.BlockSpec(memory_space=pl.ANY)
        vmem = pl.BlockSpec(memory_space=pltpu.VMEM)
        dma = pltpu.SemaphoreType.DMA
        flat = rows % 128 == 0
        router = (eb * nb, rows * nz) if flat else (nz, eb * nb, rows)
        f32, bf16 = jnp.float32, jnp.bfloat16
        landed = pl.pallas_call(
            functools.partial(kernel, nz, nb, head),
            out_shape=(
                pltpu.VMEM((2, experts, rows * nz, cb), bf16),
                pltpu.VMEM((2, experts, cb), f32),
                pltpu.VMEM(router, bf16),
            ),
            in_specs=[anyspace] * 7,
            out_specs=(vmem, vmem, vmem),
            scratch_shapes=[
                pltpu.SMEM((experts,), f32),
                pltpu.VMEM((eb, rows), f32),
                pltpu.VMEM((1, rows), f32),
                pltpu.VMEM((head + RING, 2, 2, rows, columns), f32),
                pltpu.VMEM((2, nz, experts, rows, cb), bf16),
                pltpu.VMEM((head, 2, nz, cb), f32),
                pltpu.VMEM((head, nz - 1, 2, nz, cb), f32),
                pltpu.VMEM((head, 2, nz, cb), f32),
                pltpu.VMEM((2, nh, stat, cb), f32),
                pltpu.VMEM((nh - 1, 2, stat, cb), f32),
                pltpu.VMEM((2, stat, cb), f32),
                pltpu.VMEM((2, stat, cb), f32),
                pltpu.VMEM((2, nh, stat, cb), f32),
                pltpu.VMEM((eb, rows), bf16),
                dma((3,)),
                dma((head + RING,)),
                dma((head,)),
                dma((head,)),
                dma((3,)),
                dma((3,)),
                dma,
                dma,
                dma((3,)),
                dma((3,)),
            ],
            compiler_params=pltpu.CompilerParams(
                collective_id=0, has_side_effects=True, vmem_limit_bytes=41_000_000
            ),
        )(mix_share, w_gate, avg_gate, w_up, avg_up, router_weight.T, router_gain[None, :])
        out = jax.ShapeDtypeStruct((experts, rows * nz, cb), bf16)
        scale = jax.ShapeDtypeStruct((experts, cb), f32)
        sg, su, cg, cu, rt = pl.pallas_call(
            settle,
            out_shape=(out, out, scale, scale, jax.ShapeDtypeStruct(router, bf16)),
            in_specs=[vmem] * 3,
            out_specs=(anyspace,) * 5,
            scratch_shapes=[dma((5,))],
            compiler_params=pltpu.CompilerParams(vmem_limit_bytes=4_000_000),
        )(*landed)
        rt = rt.T if flat else rt.transpose(0, 2, 1).reshape(nz * rows, nb * eb)
        return sg, su, cg, cu, rt

    whole = P("bank", "zero", None)
    served = P("bank", None, "zero")
    in_specs = (whole, whole, whole, whole, P("bank"), P("zero", "bank"), P("zero"))
    out_specs = (served, served, P("bank", "zero"), P("bank", "zero"), P())
    return jax.shard_map(
        on_device, mesh=mesh, in_specs=in_specs, out_specs=out_specs, check_vma=False
    )
```

time: 396 us -> 380 us (0.960)
  Pallas kernels: 395 us -> 379 us
    pallas_call x2, Pallas kernels: 395 us -> 379 us  [the longest x1 373 us: on_device(): pl.pallas_call(functools.partial(kernel, nz, nb, head), out_shape=(pltpu....]
where the time goes in v1:
time: 380 us; the launch traced here: 379 us
  Pallas kernels  379 us (100%)
    pallas_call x1, Pallas kernels, on_device(): pl.pallas_call(functools.partial(kernel, nz, nb, head), out_shape=(pltpu....  373 us

profile of v1, /device:TPU:8, one launch (start us, length us, event | category | flops | bytes accessed | tf_op | source)
XLA Modules:
  0.0 379.5 jit_solution(13202090462411625243)
XLA Ops:
  0.6 372.9 %shard_map.110 = (bf16[2,16,2048,128]{3,2,1,0:T(8,128)(2,1)S(1)}, f32[2,16,128]{2,1,0:T(8,128)S(1)}, bf16[64,2048]{1,0:T(8,128)(2,1)S(1)}) custom-call(f32[16]{0:T(128)} %mix_in.1, f32[16,256,1024]{2,1,0:T(8,128)} %wg.1, f32[16,256,1024]{2,1,0:T(8,128)} %ag.1, f32[16,256,1024]{2,1,0:T(8,128)} %wu.1, f32[16,256,1024]{2,1,0:T(8,128)} %au.1, ...), custom_call_target="tpu_custom_call" | custom-call | tf_op jit(solution)/shard_map/pallas_call | solution.py:277
  373.6 5.9 %shard_map.111 = (bf16[16,2048,128]{2,1,0:T(8,128)(2,1)}, bf16[16,2048,128]{2,1,0:T(8,128)(2,1)}, f32[16,128]{1,0:T(8,128)}, f32[16,128]{1,0:T(8,128)}, bf16[64,2048]{1,0:T(8,128)(2,1)}) custom-call(bf16[2,16,2048,128]{3,2,1,0:T(8,128)(2,1)S(1)} %get-tuple-element.13.land, f32[2,16,128]{2,1,0:T(8,128)S(1)} %get-tuple-element.14.scl, ...), custom_call_target="tpu_custom_call" | custom-call | tf_op jit(solution)/shard_map/pallas_call | solution.py:318

commit v2 on v1

--- a/solution.py
+++ b/solution.py
@@ -26,7 +26,7 @@
     nz, nb, head,
     mix_in, wg, ag, wu, au, rw_in, gain_in,
     land, scl, rt,
-    mix, rw, gain, stage, send, pa, ra, sa, part, rs, half, other, sb, rtp,
+    mix, rw, gain, stage, send, pa, ra, sa, part, rs, half, other, sb, rtp, raw, came,
     small_sem, in_sem, pa_ssem, pa_rsem, step_ssem, step_rsem, bulk_ssem, bulk_rsem, r_ssem, r_rsem,
 ):
     me = lax.axis_index("zero")
@@ -42,13 +42,15 @@
     inner, far = peers[:nh - 1], peers[nh - 1]
     banks = [partner(bank, k, nb) for k in range(1, nb)]
 
+    early = came.shape[0]
+
     def loads(e, slot):
         for m in range(2):
             for i, source in enumerate((ws[m], avgs[m])):
-                pltpu.make_async_copy(source.at[e], stage.at[slot, m, i], in_sem.at[slot]).start()
-
-    def loaded(slot):
-        pltpu.make_async_copy(stage.at[slot], stage.at[slot], in_sem.at[slot]).wait()
+                pltpu.make_async_copy(source.at[e], stage.at[slot, m, i], in_sem.at[slot, m]).start()
+
+    def loaded(slot, m):
+        pltpu.make_async_copy(stage.at[slot, m], stage.at[slot, m], in_sem.at[slot, m]).wait()
 
     def to(p, source, target, ssem, rsem):
         pltpu.make_async_remote_copy(
@@ -63,8 +65,7 @@
         pltpu.make_async_copy(gain_in, gain, small_sem.at[2]),
     ]
     small[0].start()
-    for e in range(head):
-        loads(e, e)
+    loads(0, 0)
 
     barrier = pltpu.get_barrier_semaphore()
     for p in peers:
@@ -94,24 +95,11 @@
         sums = lax.fori_loop(0, rows // STEP, body, tuple(jnp.zeros((8, cb), jnp.float32) for _ in range(nz)))
         return [jnp.sum(s, axis=0, keepdims=True) for s in sums]
 
-    def head_sizes(e):
-        loaded(e)
+    def sizes_to_part(slot, e, row, step):
         for m in range(2):
-            for d, size in enumerate(sizes_of(e, e, m)):
-                pa[e, m, d:d + 1, :] = size
-
-    def head_send(e):
-        for k, p in enumerate(peers):
-            to(p, pa.at[e], ra.at[e, k], pa_ssem.at[e], pa_rsem.at[e])
-
-    def head_scale(e):
-        sent(ra.at[e], pa_rsem.at[e])
-        total = pa[e]
-        for k in range(nz - 1):
-            total = total + ra[e, k]
-        sa[e] = total / (rows * nz)
-        for m in range(2):
-            scl[m, e:e + 1, :] = sa[e, m, pl.ds(me, 1), :]
+            loaded(slot, m)
+            for d, size in enumerate(sizes_of(slot, e, m)):
+                part[d // nh, d % nh, pl.ds(row + m * step, 1), :] = size
 
     place = pl.ds(pl.multiple_of(me * rows, rows), rows)
 
@@ -126,17 +114,22 @@
 
         lax.fori_loop(0, rows // STEP, body, 0)
 
-    def push(e, m):
+    def push(e, m, group=2):
         land[m, e, place, :] = send[m, me, e]
         for p in peers:
-            to(p, send.at[m, p, e], land.at[m, e, place], bulk_ssem, bulk_rsem)
+            to(p, send.at[m, p, e], land.at[m, e, place], bulk_ssem.at[group], bulk_rsem.at[group])
+
+    def push_part(i):
+        span = pl.ds(i * early, early)
+        target = pl.ds(pl.multiple_of(me * rows + i * early, early), early)
+        land[0, 0, target, :] = send[0, me, 0, span, :]
+        for k, p in enumerate(peers):
+            if i or k != bound:
+                to(p, send.at[0, p, 0, span], land.at[0, 0, target], bulk_ssem.at[i + 3], bulk_rsem.at[i + 3])
 
     def tail_sizes(i, carry):
         e = head + i
-        loaded(ring(i))
-        for m in range(2):
-            for d, size in enumerate(sizes_of(ring(i), e, m)):
-                part[d // nh, d % nh, pl.ds(m * tail + i, 1), :] = size
+        sizes_to_part(ring(i), e, 8 + i, tail)
 
         @pl.when(i + RING < tail)
         def _():
@@ -144,12 +137,74 @@
 
         return carry
 
+    spans = (pl.ds(0, 8), pl.ds(8, part.shape[2] - 8))
+
+    def step_in(g):
+        for k, p in enumerate(inner):
+            to(p, part.at[:, lax.rem(p, nh), spans[g]], rs.at[k, :, spans[g]], step_ssem.at[g, 0], step_rsem.at[g, 0])
+
+    def step_far(g):
+        sent(rs.at[:, :, spans[g]], step_rsem.at[g, 0])
+        total = part[:, near, spans[g], :]
+        for k in range(nh - 1):
+            total = total + rs[k, :, spans[g], :]
+        half[:, spans[g], :] = total
+        to(far, half.at[:, spans[g]], other.at[:, spans[g]], step_ssem.at[g, 1], step_rsem.at[g, 1])
+
+    def step_out(g):
+        sent(other.at[:, spans[g]], step_rsem.at[g, 1])
+        sb[:, near, spans[g], :] = (half[:, spans[g], :] + other[:, spans[g], :]) / (rows * nz)
+        for m in range(2):
+            if g == 0:
+                scl[m, 1:head, :] = sb[me // nh, near, m * (head - 1):(m + 1) * (head - 1), :]
+            else:
+                scl[m, head:, :] = sb[me // nh, near, 8 + m * tail:8 + (m + 1) * tail, :]
+        for p in inner:
+            to(p, sb.at[:, near, spans[g]], sb.at[:, near, spans[g]], step_ssem.at[g, 2], step_rsem.at[g, 2])
+
+    def step_done(g):
+        sent(rs.at[:, :, spans[g]], step_rsem.at[g, 2])
+
+    bound = max(nz - 3, 0)
+
     small[0].wait()
-    head_sizes(0)
+    loaded(0, 0)
+    for e in range(1, head):
+        loads(e, e)
     for i in range(min(RING, tail)):
         loads(head + i, ring(i))
-    pl.semaphore_wait(barrier, nz - 1 + nb - 1)
+
+    def head_send(m):
+        for d, size in enumerate(sizes_of(0, 0, m)):
+            pa[m, d:d + 1, :] = size
+        if m == 0:
+            pl.semaphore_wait(barrier, nz - 1 + nb - 1)
+        for k, p in enumerate(peers):
+            to(p, pa.at[m], ra.at[k, m], pa_ssem.at[m], pa_rsem.at[m])
+
+    def head_scale(m):
+        sent(ra.at[:, m], pa_rsem.at[m])
+        total = pa[m]
+        for k in range(nz - 1):
+            total = total + ra[k, m]
+        sa[m] = total / (rows * nz)
+        scl[m, 0:1, :] = sa[m, pl.ds(me, 1), :]
+
+    def keep(i, carry):
+        span = pl.ds(pl.multiple_of(i * 16, 16), 16)
+        for d in range(nz):
+            raw[d, span, :] = fresh(0, 0, 0, d, span)
+        return carry
+
     head_send(0)
+    lax.fori_loop(0, early // 16, keep, 0)
+    to(peers[bound], raw.at[peers[bound]], came, bulk_ssem.at[1], bulk_rsem.at[1])
+    loaded(0, 1)
+    head_send(1)
+    part[...] = jnp.zeros_like(part)
+    for e in range(1, head):
+        sizes_to_part(e, e, e - 1, head - 1)
+    step_in(0)
     for c in small[1:]:
         c.wait()
     rtp[...] = (rw[...] * gain[...]).astype(rtp.dtype)
@@ -169,60 +224,51 @@
         column = rt.at[:, band]
         others = rt.at[:, pl.ds(0, (nb - 1) * eb)]
         rt[me, band] = rtp[...]
+
+    head_scale(0)
+    narrow(0, 0, 0, lambda m, d: sa[m, d:d + 1, :])
+    push_part(0)
+    step_far(0)
+    push_part(1)
+    head_scale(1)
+    narrow(0, 0, 1, lambda m, d: sa[m, d:d + 1, :])
     to(far, rtp, mine, r_ssem.at[0], r_rsem.at[0])
-    for e in range(1, head):
-        head_sizes(e)
-        head_send(e)
-    part[:, :, 2 * tail:, :] = jnp.zeros_like(part[:, :, 2 * tail:, :])
-
-    for e in range(head):
-        head_scale(e)
-        for m in range(2):
-            narrow(e, e, m, lambda m, d, e=e: sa[e, m, d:d + 1, :])
-            if e == 0:
-                push(e, m)
-    lax.fori_loop(0, tail, tail_sizes, 0)
-
-    for k, p in enumerate(inner):
-        to(p, part.at[:, lax.rem(p, nh)], rs.at[k], step_ssem.at[0], step_rsem.at[0])
-    push(1, 0)
+
+    def serve_head(e, m):
+        narrow(e, e, m, lambda m, d: sb[d // nh, d % nh, pl.ds(m * (head - 1) + e - 1, 1), :])
+        push(e, m)
+
+    lax.fori_loop(0, tail // 3, tail_sizes, 0)
+    step_out(0)
+    push(0, 1, 0)
+    lax.fori_loop(tail // 3, 2 * tail // 3, tail_sizes, 0)
+    step_done(0)
+    serve_head(1, 0)
+    lax.fori_loop(2 * tail // 3, tail, tail_sizes, 0)
+    step_in(1)
     for i in range(min(RING, tail)):
         loads(head + i, ring(i))
+    serve_head(1, 1)
+    step_far(1)
+    serve_head(2, 0)
+    step_out(1)
     pltpu.make_async_copy(theirs, theirs, r_rsem.at[0]).wait()
     for p in inner:
         for tile in (mine, theirs):
             to(p, tile, tile, r_ssem.at[1], r_rsem.at[1])
-
-    sent(rs, step_rsem.at[0])
-    total = part[:, near]
-    for k in range(nh - 1):
-        total = total + rs[k]
-    half[...] = total
-    to(far, half, other, step_ssem.at[1], step_rsem.at[1])
-    push(1, 1)
-
-    sent(other, step_rsem.at[1])
-    total = (half[...] + other[...]) / (rows * nz)
-    sb[:, near] = total
-    for m in range(2):
-        scl[m, head:, :] = sb[me // nh, near, m * tail:(m + 1) * tail, :]
-    for p in inner:
-        to(p, sb.at[:, near], sb.at[:, near], step_ssem.at[2], step_rsem.at[2])
-    for e in range(2, head):
-        for m in range(2):
-            push(e, m)
+    serve_head(2, 1)
 
     sent(tiles, r_rsem.at[1])
     for p in banks:
         pltpu.make_async_remote_copy(
             column, column, r_ssem.at[2], r_rsem.at[2], device_id={"bank": p}, device_id_type=MESH).start()
-    sent(rs, step_rsem.at[2])
+    step_done(1)
 
     def serve(i, carry):
         e = head + i
-        loaded(ring(i))
         for m in range(2):
-            narrow(ring(i), e, m, lambda m, d: sb[d // nh, d % nh, pl.ds(m * tail + i, 1), :])
+            loaded(ring(i), m)
+            narrow(ring(i), e, m, lambda m, d: sb[d // nh, d % nh, pl.ds(8 + m * tail + i, 1), :])
             push(e, m)
 
         @pl.when(i + RING < tail)
@@ -233,17 +279,32 @@
 
     lax.fori_loop(0, tail, serve, 0)
 
-    for e in range(head):
-        sent(ra.at[e], pa_ssem.at[e])
-    sent(rs, step_ssem.at[0])
-    sent(other, step_ssem.at[1])
-    sent(rs, step_ssem.at[2])
+    sent(came, bulk_rsem.at[1])
+    inverse = 1.0 / sa[0, pl.ds(me, 1), :]
+
+    def widen(i, carry):
+        span = pl.ds(pl.multiple_of(i * 16, 16), 16)
+        rest = pl.ds(pl.multiple_of(peers[bound] * rows + i * 16, 16), 16)
+        land[0, 0, rest, :] = (came[span, :] * inverse).astype(land.dtype)
+        return carry
+
+    lax.fori_loop(0, early // 16, widen, 0)
+    sent(came, bulk_ssem.at[1])
+    for m in range(2):
+        sent(ra.at[:, m], pa_ssem.at[m])
+    for g in range(2):
+        sent(rs.at[:, :, spans[g]], step_ssem.at[g, 0])
+        sent(other.at[:, spans[g]], step_ssem.at[g, 1])
+        sent(rs.at[:, :, spans[g]], step_ssem.at[g, 2])
     sent(rtp, r_ssem.at[0])
     sent(tiles, r_ssem.at[1])
     for sem in (r_ssem, r_rsem):
         sent(others, sem.at[2])
-    sent(send.at[:, pl.ds(0, nz - 1)], bulk_ssem)
-    sent(land.at[:, :, pl.ds(0, (nz - 1) * rows)], bulk_rsem)
+    for sems in (bulk_ssem, bulk_rsem):
+        sent(land.at[1, 0, pl.ds(0, (nz - 1) * rows)], sems.at[0])
+        sent(land.at[:, pl.ds(1, experts - 1), pl.ds(0, (nz - 1) * rows)], sems.at[2])
+        sent(land.at[0, 0, pl.ds(0, (nz - 2) * early)], sems.at[3])
+        sent(land.at[0, 0, pl.ds(0, (nz - 1) * early)], sems.at[4])
 
 
 def settle(land, scl, rt, og, ou, sg, su, out, sem):
@@ -266,8 +327,9 @@
         cb = columns // nz
         eb = router_weight.shape[1]
         nh = nz // 2
-        head = min(HEAD, experts - 1)
-        stat = (2 * (experts - head) // 8 + 1) * 8
+        head = min(HEAD, experts)
+        stat = 8 + (2 * (experts - head) // 8 + 1) * 8
+        early = rows // 2
         anyspace = pl.BlockSpec(memory_space=pl.ANY)
         vmem = pl.BlockSpec(memory_space=pltpu.VMEM)
         dma = pltpu.SemaphoreType.DMA
@@ -289,28 +351,30 @@
                 pltpu.VMEM((1, rows), f32),
                 pltpu.VMEM((head + RING, 2, 2, rows, columns), f32),
                 pltpu.VMEM((2, nz, experts, rows, cb), bf16),
-                pltpu.VMEM((head, 2, nz, cb), f32),
-                pltpu.VMEM((head, nz - 1, 2, nz, cb), f32),
-                pltpu.VMEM((head, 2, nz, cb), f32),
+                pltpu.VMEM((2, nz, cb), f32),
+                pltpu.VMEM((nz - 1, 2, nz, cb), f32),
+                pltpu.VMEM((2, nz, cb), f32),
                 pltpu.VMEM((2, nh, stat, cb), f32),
                 pltpu.VMEM((nh - 1, 2, stat, cb), f32),
                 pltpu.VMEM((2, stat, cb), f32),
                 pltpu.VMEM((2, stat, cb), f32),
                 pltpu.VMEM((2, nh, stat, cb), f32),
                 pltpu.VMEM((eb, rows), bf16),
+                pltpu.VMEM((nz, early, cb), f32),
+                pltpu.VMEM((early, cb), f32),
                 dma((3,)),
-                dma((head + RING,)),
-                dma((head,)),
-                dma((head,)),
-                dma((3,)),
-                dma((3,)),
-                dma,
-                dma,
+                dma((head + RING, 2)),
+                dma((2,)),
+                dma((2,)),
+                dma((2, 3)),
+                dma((2, 3)),
+                dma((5,)),
+                dma((5,)),
                 dma((3,)),
                 dma((3,)),
             ],
             compiler_params=pltpu.CompilerParams(
-                collective_id=0, has_side_effects=True, vmem_limit_bytes=41_000_000
+                collective_id=0, has_side_effects=True, vmem_limit_bytes=44_000_000
             ),
         )(mix_share, w_gate, avg_gate, w_up, avg_up, router_weight.T, router_gain[None, :])
         out = jax.ShapeDtypeStruct((experts, rows * nz, cb), bf16)

time: 380 us -> 378 us (level)
  no operation moved by 1% of the time
where the time goes in v2:
time: 378 us
  Pallas kernels  377 us (100%)
    pallas_call x1, Pallas kernels, on_device(): pl.pallas_call(functools.partial(kernel, nz, nb, head), out_shape=(pltpu....  371 us

profile of v2, /device:TPU:8, one launch (start us, length us, event | category | flops | bytes accessed | tf_op | source)
XLA Modules:
  0.0 377.6 jit_solution(3349503471083033111)
XLA Ops:
  0.6 371.1 %shard_map.110 = (bf16[2,16,2048,128]{3,2,1,0:T(8,128)(2,1)S(1)}, f32[2,16,128]{2,1,0:T(8,128)S(1)}, bf16[64,2048]{1,0:T(8,128)(2,1)S(1)}) custom-call(f32[16]{0:T(128)} %mix_in.1, f32[16,256,1024]{2,1,0:T(8,128)} %wg.1, f32[16,256,1024]{2,1,0:T(8,128)} %ag.1, f32[16,256,1024]{2,1,0:T(8,128)} %wu.1, f32[16,256,1024]{2,1,0:T(8,128)} %au.1, ...), custom_call_target="tpu_custom_call" | custom-call | tf_op jit(solution)/shard_map/pallas_call | solution.py:339
  371.7 5.9 %shard_map.111 = (bf16[16,2048,128]{2,1,0:T(8,128)(2,1)}, bf16[16,2048,128]{2,1,0:T(8,128)(2,1)}, f32[16,128]{1,0:T(8,128)}, f32[16,128]{1,0:T(8,128)}, bf16[64,2048]{1,0:T(8,128)(2,1)}) custom-call(bf16[2,16,2048,128]{3,2,1,0:T(8,128)(2,1)S(1)} %get-tuple-element.13.land, f32[2,16,128]{2,1,0:T(8,128)S(1)} %get-tuple-element.14.scl, ...), custom_call_target="tpu_custom_call" | custom-call | tf_op jit(solution)/shard_map/pallas_call | solution.py:382

commit v3 on v2

--- a/solution.py
+++ b/solution.py
@@ -120,8 +120,9 @@
             to(p, send.at[m, p, e], land.at[m, e, place], bulk_ssem.at[group], bulk_rsem.at[group])
 
     def push_part(i):
-        span = pl.ds(i * early, early)
-        target = pl.ds(pl.multiple_of(me * rows + i * early, early), early)
+        lo, n = (early, rows - early) if i else (0, early)
+        span = pl.ds(lo, n)
+        target = pl.ds(pl.multiple_of(me * rows + lo, 16), n)
         land[0, 0, target, :] = send[0, me, 0, span, :]
         for k, p in enumerate(peers):
             if i or k != bound:
@@ -277,7 +278,15 @@
 
         return carry
 
-    lax.fori_loop(0, tail, serve, 0)
+    lax.fori_loop(0, tail - 1, serve, 0)
+    e = experts - 1
+    for m in range(2):
+        loaded(ring(tail - 1), m)
+        narrow(ring(tail - 1), e, m, lambda m, d: sb[d // nh, d % nh, pl.ds(8 + (m + 1) * tail - 1, 1), :])
+        land[m, e, place, :] = send[m, me, e]
+    for p in peers:
+        for m in range(2):
+            to(p, send.at[m, p, e], land.at[m, e, place], bulk_ssem.at[2], bulk_rsem.at[2])
 
     sent(came, bulk_rsem.at[1])
     inverse = 1.0 / sa[0, pl.ds(me, 1), :]
@@ -304,7 +313,7 @@
         sent(land.at[1, 0, pl.ds(0, (nz - 1) * rows)], sems.at[0])
         sent(land.at[:, pl.ds(1, experts - 1), pl.ds(0, (nz - 1) * rows)], sems.at[2])
         sent(land.at[0, 0, pl.ds(0, (nz - 2) * early)], sems.at[3])
-        sent(land.at[0, 0, pl.ds(0, (nz - 1) * early)], sems.at[4])
+        sent(land.at[0, 0, pl.ds(0, (nz - 1) * (rows - early))], sems.at[4])
 
 
 def settle(land, scl, rt, og, ou, sg, su, out, sem):
@@ -329,7 +338,7 @@
         nh = nz // 2
         head = min(HEAD, experts)
         stat = 8 + (2 * (experts - head) // 8 + 1) * 8
-        early = rows // 2
+        early = rows * 3 // 4 // 16 * 16
         anyspace = pl.BlockSpec(memory_space=pl.ANY)
         vmem = pl.BlockSpec(memory_space=pltpu.VMEM)
         dma = pltpu.SemaphoreType.DMA

time: 378 us -> 377 us (level)
  no operation moved by 1% of the time
where the time goes in v3:
time: 377 us
  Pallas kernels  377 us (100%)
    pallas_call x1, Pallas kernels, on_device(): pl.pallas_call(functools.partial(kernel, nz, nb, head), out_shape=(pltpu....  371 us

profile of v3, /device:TPU:8, one launch (start us, length us, event | category | flops | bytes accessed | tf_op | source)
XLA Modules:
  0.0 377.3 jit_solution(6205441663218277994)
XLA Ops:
  0.6 370.7 %shard_map.110 = (bf16[2,16,2048,128]{3,2,1,0:T(8,128)(2,1)S(1)}, f32[2,16,128]{2,1,0:T(8,128)S(1)}, bf16[64,2048]{1,0:T(8,128)(2,1)S(1)}) custom-call(f32[16]{0:T(128)} %mix_in.1, f32[16,256,1024]{2,1,0:T(8,128)} %wg.1, f32[16,256,1024]{2,1,0:T(8,128)} %ag.1, f32[16,256,1024]{2,1,0:T(8,128)} %wu.1, f32[16,256,1024]{2,1,0:T(8,128)} %au.1, ...), custom_call_target="tpu_custom_call" | custom-call | tf_op jit(solution)/shard_map/pallas_call | solution.py:348
  371.4 5.9 %shard_map.111 = (bf16[16,2048,128]{2,1,0:T(8,128)(2,1)}, bf16[16,2048,128]{2,1,0:T(8,128)(2,1)}, f32[16,128]{1,0:T(8,128)}, f32[16,128]{1,0:T(8,128)}, bf16[64,2048]{1,0:T(8,128)(2,1)}) custom-call(bf16[2,16,2048,128]{3,2,1,0:T(8,128)(2,1)S(1)} %get-tuple-element.13.land, f32[2,16,128]{2,1,0:T(8,128)S(1)} %get-tuple-element.14.scl, ...), custom_call_target="tpu_custom_call" | custom-call | tf_op jit(solution)/shard_map/pallas_call | solution.py:391

commit v4 on v3

--- a/solution.py
+++ b/solution.py
@@ -103,7 +103,7 @@
 
     place = pl.ds(pl.multiple_of(me * rows, rows), rows)
 
-    def narrow(slot, e, m, scale):
+    def narrow(slot, e, m, scale, lo=0, hi=None):
         inverses = [1.0 / scale(m, d) for d in range(nz)]
 
         def body(i, carry):
@@ -112,7 +112,7 @@
                 send[m, d, e, span, :] = (fresh(slot, e, m, d, span) * inverses[d]).astype(send.dtype)
             return carry
 
-        lax.fori_loop(0, rows // STEP, body, 0)
+        lax.fori_loop(lo, rows // STEP if hi is None else hi, body, 0)
 
     def push(e, m, group=2):
         land[m, e, place, :] = send[m, me, e]
@@ -227,8 +227,10 @@
         rt[me, band] = rtp[...]
 
     head_scale(0)
-    narrow(0, 0, 0, lambda m, d: sa[m, d:d + 1, :])
+    cut = -(-early // STEP)
+    narrow(0, 0, 0, lambda m, d: sa[m, d:d + 1, :], 0, cut)
     push_part(0)
+    narrow(0, 0, 0, lambda m, d: sa[m, d:d + 1, :], cut)
     step_far(0)
     push_part(1)
     head_scale(1)
@@ -337,7 +339,7 @@
         eb = router_weight.shape[1]
         nh = nz // 2
         head = min(HEAD, experts)
-        stat = 8 + (2 * (experts - head) // 8 + 1) * 8
+        stat = 8 + 2 * (experts - head)
         early = rows * 3 // 4 // 16 * 16
         anyspace = pl.BlockSpec(memory_space=pl.ANY)
         vmem = pl.BlockSpec(memory_space=pltpu.VMEM)

time: 377 us -> 377 us (level)
  no operation moved by 1% of the time
where the time goes in v4:
time: 377 us
  Pallas kernels  376 us (100%)
    pallas_call x1, Pallas kernels, on_device(): pl.pallas_call(functools.partial(kernel, nz, nb, head), out_shape=(pltpu....  370 us

profile of v4, /device:TPU:8, one launch (start us, length us, event | category | flops | bytes accessed | tf_op | source)
XLA Modules:
  0.0 377.0 jit_solution(8548012698441809065)
XLA Ops:
  0.6 370.5 %shard_map.110 = (bf16[2,16,2048,128]{3,2,1,0:T(8,128)(2,1)S(1)}, f32[2,16,128]{2,1,0:T(8,128)S(1)}, bf16[64,2048]{1,0:T(8,128)(2,1)S(1)}) custom-call(f32[16]{0:T(128)} %mix_in.1, f32[16,256,1024]{2,1,0:T(8,128)} %wg.1, f32[16,256,1024]{2,1,0:T(8,128)} %ag.1, f32[16,256,1024]{2,1,0:T(8,128)} %wu.1, f32[16,256,1024]{2,1,0:T(8,128)} %au.1, ...), custom_call_target="tpu_custom_call" | custom-call | tf_op jit(solution)/shard_map/pallas_call | solution.py:350
  371.1 5.9 %shard_map.111 = (bf16[16,2048,128]{2,1,0:T(8,128)(2,1)}, bf16[16,2048,128]{2,1,0:T(8,128)(2,1)}, f32[16,128]{1,0:T(8,128)}, f32[16,128]{1,0:T(8,128)}, bf16[64,2048]{1,0:T(8,128)(2,1)}) custom-call(bf16[2,16,2048,128]{3,2,1,0:T(8,128)(2,1)S(1)} %get-tuple-element.13.land, f32[2,16,128]{2,1,0:T(8,128)S(1)} %get-tuple-element.14.scl, ...), custom_call_target="tpu_custom_call" | custom-call | tf_op jit(solution)/shard_map/pallas_call | solution.py:393
